TPU v7x, 128 devices: a whole 4x4x4 slice. The times are simulated.
128 devices in a mesh: seq: 32 (over z_lo, y, x), head: 4 (over z_hi, core).
Axes of the slice: x: 4, y: 4, z: 4 (z_hi: 2, z_lo: 2; z = z_hi * 2 + z_lo), core: 2. Of those that a mesh axis runs over, the one named last changes fastest.
Arguments:
- text_states: bfloat16 [8192, 4096], P('seq', 'head'), may hold values from -200 to 200
- query_weight: bfloat16 [4096, 4096], P(None, 'head'), may hold values from -0.09375 to 0.09375
- image_keys: bfloat16 [16384, 1024], P('seq', 'head'), may hold values from -12 to 12
- image_values: bfloat16 [16384, 1024], P('seq', 'head'), may hold values from -24 to 24
- output_weight: bfloat16 [4096, 4096], P('head'), may hold values from -0.09375 to 0.09375
- attn_gate: float32 [1], replicated, may hold values from 0.3 to 1.5
- frame_lengths: int32 [64], replicated, may hold values from 1 to 512, 16384 in all
- frame_limit: int32 [128], replicated, may hold values from 0 to 64
Outputs:
- gated_branch: bfloat16 [8192, 4096], P('seq', 'head')
Inputs may be any that keep to these rules, and one draw needn't show every extreme that they name: `frame_lengths`: the lengths sum to 16384.
All inputs are finite; a program needn't handle non-finite values.
Results may differ from a plain program's by a relative error of at most 0.014.
The roundings to bfloat16 on the way count: a program that leaves them out, or rounds other values in their place, can miss the bound.
Values may be sent and summed in bfloat16 or wider, within the bound.
A program may use at most 128 MiB of HBM per device.

v0:
```python
import math

import jax
import jax.numpy as jnp
from jax import lax
from jax.sharding import PartitionSpec as P

HD = 128
TBLK = 64
GROUP = 4


masked_fill = -1e30


def from_everyone(x, axis):
    copies = jnp.broadcast_to(x, (lax.axis_size(axis), *x.shape))
    return lax.all_to_all(copies, axis, split_axis=0, concat_axis=0, tiled=True)


def in_order(tiles, dim):
    dims = list(tiles.shape[1:])
    dims[dim] *= tiles.shape[0]
    return jnp.moveaxis(tiles, 0, dim).reshape(dims)


def gathered_copies(x, axis, dim):
    tiles = from_everyone(x, axis)
    return in_order(tiles, dim)


def from_behind(block, axis, distance):
    devices = range(lax.axis_size(axis))
    route = [((i - distance) % len(devices), i) for i in devices]
    return lax.ppermute(block, axis, route)


def in_blocks(x, dim, peers):
    before, after = (x.shape[:dim], x.shape[dim + 1 :])
    return jnp.moveaxis(x.reshape(*before, peers, -1, *after), dim, 0)


def sent_and_summed(x, axis, dim):
    tiles = in_blocks(x, dim, lax.axis_size(axis))
    arrived = lax.all_to_all(tiles, axis, split_axis=0, concat_axis=0, tiled=True)
    return arrived.astype(jnp.float32).sum(axis=0)


def shards(
    text_states,
    query_weight,
    image_keys,
    image_values,
    output_weight,
    attn_gate,
    frame_lengths,
    frame_limit,
):
    text_rows = text_states.shape[0]
    video_rows = image_keys.shape[0]
    local_kv = image_keys.shape[1] // HD
    seq_index = lax.axis_index("seq")
    cycle_size = lax.axis_size("seq")
    score_scale = 1.0 / math.sqrt(HD)
    queries = jnp.dot(
        gathered_copies(text_states, "head", 1), query_weight, preferred_element_type=jnp.float32
    ).astype(jnp.bfloat16)
    grouped_queries = (
        queries.reshape(text_rows, local_kv, GROUP, HD)
        .transpose(1, 2, 0, 3)
        .reshape(local_kv, GROUP * text_rows, HD)
    )
    frame_ends = jnp.cumsum(frame_lengths)
    block_count = text_rows // TBLK
    my_limits = lax.dynamic_slice_in_dim(frame_limit, seq_index * block_count, block_count, 0)
    group_limits = jnp.tile(jnp.repeat(my_limits, TBLK), GROUP)

    def dense_block(running, key_block, value_block, key_frames):
        best_score, weight_sum, accumulated = running
        key_head_count = key_block.reshape(key_block.shape[0], local_kv, HD)
        value_heads = value_block.reshape(value_block.shape[0], local_kv, HD)
        scores = (
            jnp.einsum(
                "sxn,lsn->sxl", grouped_queries, key_head_count, preferred_element_type=jnp.float32
            )
            * score_scale
        )
        visible = key_frames[None, None, :] < group_limits[None, :, None]
        block_best = jnp.max(jnp.where(visible, scores, masked_fill), axis=2)
        new_best = jnp.maximum(best_score, block_best)
        weights = jnp.where(visible, jnp.exp(scores - new_best[:, :, None]), 0.0)
        factor = jnp.exp(best_score - new_best)
        weight_sum = weight_sum * factor + jnp.sum(weights, axis=2)
        mixed = jnp.einsum(
            "vus,svg->vug",
            weights.astype(jnp.bfloat16),
            value_heads,
            preferred_element_type=jnp.float32,
        )
        accumulated = accumulated * factor[:, :, None] + mixed
        return (new_best, weight_sum, accumulated)

    def attend_frames(running, key_block, value_block, first_row):
        token_positions = first_row + jnp.arange(key_block.shape[0], dtype=jnp.int32)
        key_frames = jnp.sum(
            (frame_ends[None, :] <= token_positions[:, None]).astype(jnp.int32), axis=1
        )
        return dense_block(running, key_block, value_block, key_frames)

    initial = (
        jnp.full((local_kv, GROUP * text_rows), masked_fill, jnp.float32),
        jnp.zeros((local_kv, GROUP * text_rows), jnp.float32),
        jnp.zeros((local_kv, GROUP * text_rows, HD), jnp.float32),
    )
    half_rows = video_rows // 2

    def paired_turn(turn_index, state_in):
        running, keys_up, values_up, keys_down, values_down = state_in
        source_up = (seq_index - turn_index) % cycle_size
        source_down = (seq_index + turn_index) % cycle_size
        running = attend_frames(running, keys_up, values_up, source_up * video_rows)
        running = attend_frames(
            running, keys_down, values_down, source_down * video_rows + half_rows
        )
        keys_up, values_up = from_behind((keys_up, values_up), "seq", 1)
        keys_down, values_down = from_behind((keys_down, values_down), "seq", -1)
        return (running, keys_up, values_up, keys_down, values_down)

    start_state = (
        initial,
        image_keys[:half_rows],
        image_values[:half_rows],
        image_keys[half_rows:],
        image_values[half_rows:],
    )
    running, keys_up, values_up, keys_down, values_down = lax.fori_loop(
        0, cycle_size - 1, paired_turn, start_state
    )
    running = attend_frames(running, keys_up, values_up, (seq_index + 1) % cycle_size * video_rows)
    running = attend_frames(
        running, keys_down, values_down, (seq_index - 1) % cycle_size * video_rows + half_rows
    )
    best_score, weight_sum, accumulated = running
    output_groups = (accumulated / jnp.maximum(weight_sum, 1.0)[:, :, None]).astype(jnp.bfloat16)
    attention_output = (
        output_groups.reshape(local_kv, GROUP, text_rows, HD)
        .transpose(2, 0, 1, 3)
        .reshape(text_rows, local_kv * GROUP * HD)
    )
    summed = sent_and_summed(
        lax.dot_general(
            output_weight,
            attention_output,
            (((0,), (1,)), ((), ())),
            preferred_element_type=jnp.float32,
        ).astype(jnp.bfloat16),
        "head",
        0,
    )
    return (jnp.tanh(attn_gate[0]) * summed.T).astype(jnp.bfloat16)


def solution(mesh):
    in_specs = (
        P("seq", "head"),
        P(None, "head"),
        P("seq", "head"),
        P("seq", "head"),
        P("head", None),
        P(),
        P(),
        P(),
    )
    out_specs = P("seq", "head")
    return jax.shard_map(shards, mesh=mesh, in_specs=in_specs, out_specs=out_specs, check_vma=False)
```

profile of v0, /device:TPU:1, one launch (start us, length us, event | category | flops | bytes accessed | tf_op | source)
XLA Modules:
  0.0 540.5 jit_solution(9037074821098661656)
XLA Ops:
  2.7 6.8 %all-to-all-start = ((bf16[4,256,1024]{1,2,0:T(8,128)(2,1)}), bf16[4,256,1024]{1,2,0:T(8,128)(2,1)S(1)}, u32[]{:S(2)}, u32[]{:S(2)}) async-start(bf16[4,256,1024]{1,2,0:T(8,128)(2,1)} %broadcast_in_dim.152), calls=%async_computation | async-start | bytes 4194304 | tf_op jit(solution)/shard_map/all_to_all | solution.py:18
  11.6 24.1 %all-to-all-done = bf16[4,256,1024]{1,2,0:T(8,128)(2,1)S(1)} async-done(((bf16[4,256,1024]{1,2,0:T(8,128)(2,1)}), bf16[4,256,1024]{1,2,0:T(8,128)(2,1)S(1)}, u32[]{:S(2)}, u32[]{:S(2)}) %all-to-all-start) | async-done | bytes 2097184 | tf_op jit(solution)/shard_map/all_to_all | solution.py:18
  35.7 6.5 %convolution_convert_fusion.1 = bf16[256,1024]{1,0:T(8,128)(2,1)} fusion(bf16[256,4096]{0,1:T(8,128)(2,1)S(1)} %bitcast.121, bf16[4096,1024]{1,0:T(8,128)(2,1)} %param.11), kind=kOutput, calls=%fused_computation.66 | convolution fusion | flops 2147745792 | bytes 11010048 | tf_op jit(solution)/shard_map/dot_general | solution.py:65
  43.7 417.6 %while.28 = (s32[]{:T(128)}, f32[2,1024]{1,0:T(2,128)S(1)}, f32[2,1024]{1,0:T(2,128)S(1)}, f32[2,1024,128]{2,1,0:T(8,128)}, bf16[256,256]{1,0:T(8,128)(2,1)S(1)}...) while((s32[]{:T(128)}, f32[2,1024]{1,0:T(2,128)S(1)}, ...), condition=%wide.region_8.9_spmd.clone, body=%wide.region_1.8_spmd.clone.sunk | while | flops 550352896 | bytes 28026764 | solution.py:136
  46.3 4.5 collective-permute-start.2
  55.3 1.8 convolution_add_fusion.5
  58.6 5.7 %collective-permute-start.2 = (bf16[256,256]{1,0:T(8,128)(2,1)S(1)}, bf16[256,256]{1,0:T(8,128)(2,1)S(1)}, u32[]{:S(2)}, u32[]{:S(2)}) collective-permute-start(bf16[256,256]{1,0:T(8,128)(2,1)S(1)} %copy.154), channel_id=1, source_target_pairs={{4,0},{8,4},{12,8},{16,12},{20,16},{24,20},{28,24},{32,28},{36,32}... | collective-permute-start | bytes 393224 | tf_op jit(solution)/shard_map/while/body/eval_jaxpr/ppermute | solution.py:35
  68.8 1.8 convolution_add_fusion.5
  72.1 5.7 %collective-permute-start.2 = (bf16[256,256]{1,0:T(8,128)(2,1)S(1)}, bf16[256,256]{1,0:T(8,128)(2,1)S(1)}, u32[]{:S(2)}, u32[]{:S(2)}) collective-permute-start(bf16[256,256]{1,0:T(8,128)(2,1)S(1)} %copy.154), channel_id=1, source_target_pairs={{4,0},{8,4},{12,8},{16,12},{20,16},{24,20},{28,24},{32,28},{36,32}... | collective-permute-start | bytes 393224 | tf_op jit(solution)/shard_map/while/body/eval_jaxpr/ppermute | solution.py:35
  82.3 1.8 convolution_add_fusion.5
  85.5 5.7 %collective-permute-start.2 = (bf16[256,256]{1,0:T(8,128)(2,1)S(1)}, bf16[256,256]{1,0:T(8,128)(2,1)S(1)}, u32[]{:S(2)}, u32[]{:S(2)}) collective-permute-start(bf16[256,256]{1,0:T(8,128)(2,1)S(1)} %copy.154), channel_id=1, source_target_pairs={{4,0},{8,4},{12,8},{16,12},{20,16},{24,20},{28,24},{32,28},{36,32}... | collective-permute-start | bytes 393224 | tf_op jit(solution)/shard_map/while/body/eval_jaxpr/ppermute | solution.py:35
  95.7 1.8 convolution_add_fusion.5
  99.0 5.7 %collective-permute-start.2 = (bf16[256,256]{1,0:T(8,128)(2,1)S(1)}, bf16[256,256]{1,0:T(8,128)(2,1)S(1)}, u32[]{:S(2)}, u32[]{:S(2)}) collective-permute-start(bf16[256,256]{1,0:T(8,128)(2,1)S(1)} %copy.154), channel_id=1, source_target_pairs={{4,0},{8,4},{12,8},{16,12},{20,16},{24,20},{28,24},{32,28},{36,32}... | collective-permute-start | bytes 393224 | tf_op jit(solution)/shard_map/while/body/eval_jaxpr/ppermute | solution.py:35
  109.2 1.8 convolution_add_fusion.5
  112.5 5.7 %collective-permute-start.2 = (bf16[256,256]{1,0:T(8,128)(2,1)S(1)}, bf16[256,256]{1,0:T(8,128)(2,1)S(1)}, u32[]{:S(2)}, u32[]{:S(2)}) collective-permute-start(bf16[256,256]{1,0:T(8,128)(2,1)S(1)} %copy.154), channel_id=1, source_target_pairs={{4,0},{8,4},{12,8},{16,12},{20,16},{24,20},{28,24},{32,28},{36,32}... | collective-permute-start | bytes 393224 | tf_op jit(solution)/shard_map/while/body/eval_jaxpr/ppermute | solution.py:35
  122.7 1.8 convolution_add_fusion.5
  125.9 5.7 %collective-permute-start.2 = (bf16[256,256]{1,0:T(8,128)(2,1)S(1)}, bf16[256,256]{1,0:T(8,128)(2,1)S(1)}, u32[]{:S(2)}, u32[]{:S(2)}) collective-permute-start(bf16[256,256]{1,0:T(8,128)(2,1)S(1)} %copy.154), channel_id=1, source_target_pairs={{4,0},{8,4},{12,8},{16,12},{20,16},{24,20},{28,24},{32,28},{36,32}... | collective-permute-start | bytes 393224 | tf_op jit(solution)/shard_map/while/body/eval_jaxpr/ppermute | solution.py:35
  136.1 1.8 convolution_add_fusion.5
  139.4 5.7 %collective-permute-start.2 = (bf16[256,256]{1,0:T(8,128)(2,1)S(1)}, bf16[256,256]{1,0:T(8,128)(2,1)S(1)}, u32[]{:S(2)}, u32[]{:S(2)}) collective-permute-start(bf16[256,256]{1,0:T(8,128)(2,1)S(1)} %copy.154), channel_id=1, source_target_pairs={{4,0},{8,4},{12,8},{16,12},{20,16},{24,20},{28,24},{32,28},{36,32}... | collective-permute-start | bytes 393224 | tf_op jit(solution)/shard_map/while/body/eval_jaxpr/ppermute | solution.py:35
  149.6 1.8 convolution_add_fusion.5
  152.9 5.7 %collective-permute-start.2 = (bf16[256,256]{1,0:T(8,128)(2,1)S(1)}, bf16[256,256]{1,0:T(8,128)(2,1)S(1)}, u32[]{:S(2)}, u32[]{:S(2)}) collective-permute-start(bf16[256,256]{1,0:T(8,128)(2,1)S(1)} %copy.154), channel_id=1, source_target_pairs={{4,0},{8,4},{12,8},{16,12},{20,16},{24,20},{28,24},{32,28},{36,32}... | collective-permute-start | bytes 393224 | tf_op jit(solution)/shard_map/while/body/eval_jaxpr/ppermute | solution.py:35
  163.1 1.8 convolution_add_fusion.5
  166.3 5.7 %collective-permute-start.2 = (bf16[256,256]{1,0:T(8,128)(2,1)S(1)}, bf16[256,256]{1,0:T(8,128)(2,1)S(1)}, u32[]{:S(2)}, u32[]{:S(2)}) collective-permute-start(bf16[256,256]{1,0:T(8,128)(2,1)S(1)} %copy.154), channel_id=1, source_target_pairs={{4,0},{8,4},{12,8},{16,12},{20,16},{24,20},{28,24},{32,28},{36,32}... | collective-permute-start | bytes 393224 | tf_op jit(solution)/shard_map/while/body/eval_jaxpr/ppermute | solution.py:35
  176.5 1.8 convolution_add_fusion.5
  179.8 5.7 %collective-permute-start.2 = (bf16[256,256]{1,0:T(8,128)(2,1)S(1)}, bf16[256,256]{1,0:T(8,128)(2,1)S(1)}, u32[]{:S(2)}, u32[]{:S(2)}) collective-permute-start(bf16[256,256]{1,0:T(8,128)(2,1)S(1)} %copy.154), channel_id=1, source_target_pairs={{4,0},{8,4},{12,8},{16,12},{20,16},{24,20},{28,24},{32,28},{36,32}... | collective-permute-start | bytes 393224 | tf_op jit(solution)/shard_map/while/body/eval_jaxpr/ppermute | solution.py:35
  190.0 1.8 convolution_add_fusion.5
  193.3 5.7 %collective-permute-start.2 = (bf16[256,256]{1,0:T(8,128)(2,1)S(1)}, bf16[256,256]{1,0:T(8,128)(2,1)S(1)}, u32[]{:S(2)}, u32[]{:S(2)}) collective-permute-start(bf16[256,256]{1,0:T(8,128)(2,1)S(1)} %copy.154), channel_id=1, source_target_pairs={{4,0},{8,4},{12,8},{16,12},{20,16},{24,20},{28,24},{32,28},{36,32}... | collective-permute-start | bytes 393224 | tf_op jit(solution)/shard_map/while/body/eval_jaxpr/ppermute | solution.py:35
  203.5 1.8 convolution_add_fusion.5
  206.7 5.7 %collective-permute-start.2 = (bf16[256,256]{1,0:T(8,128)(2,1)S(1)}, bf16[256,256]{1,0:T(8,128)(2,1)S(1)}, u32[]{:S(2)}, u32[]{:S(2)}) collective-permute-start(bf16[256,256]{1,0:T(8,128)(2,1)S(1)} %copy.154), channel_id=1, source_target_pairs={{4,0},{8,4},{12,8},{16,12},{20,16},{24,20},{28,24},{32,28},{36,32}... | collective-permute-start | bytes 393224 | tf_op jit(solution)/shard_map/while/body/eval_jaxpr/ppermute | solution.py:35
  216.9 1.8 convolution_add_fusion.5
  220.2 5.7 %collective-permute-start.2 = (bf16[256,256]{1,0:T(8,128)(2,1)S(1)}, bf16[256,256]{1,0:T(8,128)(2,1)S(1)}, u32[]{:S(2)}, u32[]{:S(2)}) collective-permute-start(bf16[256,256]{1,0:T(8,128)(2,1)S(1)} %copy.154), channel_id=1, source_target_pairs={{4,0},{8,4},{12,8},{16,12},{20,16},{24,20},{28,24},{32,28},{36,32}... | collective-permute-start | bytes 393224 | tf_op jit(solution)/shard_map/while/body/eval_jaxpr/ppermute | solution.py:35
  230.4 1.8 convolution_add_fusion.5
  233.7 5.7 %collective-permute-start.2 = (bf16[256,256]{1,0:T(8,128)(2,1)S(1)}, bf16[256,256]{1,0:T(8,128)(2,1)S(1)}, u32[]{:S(2)}, u32[]{:S(2)}) collective-permute-start(bf16[256,256]{1,0:T(8,128)(2,1)S(1)} %copy.154), channel_id=1, source_target_pairs={{4,0},{8,4},{12,8},{16,12},{20,16},{24,20},{28,24},{32,28},{36,32}... | collective-permute-start | bytes 393224 | tf_op jit(solution)/shard_map/while/body/eval_jaxpr/ppermute | solution.py:35
  243.9 1.8 convolution_add_fusion.5
  247.1 5.7 %collective-permute-start.2 = (bf16[256,256]{1,0:T(8,128)(2,1)S(1)}, bf16[256,256]{1,0:T(8,128)(2,1)S(1)}, u32[]{:S(2)}, u32[]{:S(2)}) collective-permute-start(bf16[256,256]{1,0:T(8,128)(2,1)S(1)} %copy.154), channel_id=1, source_target_pairs={{4,0},{8,4},{12,8},{16,12},{20,16},{24,20},{28,24},{32,28},{36,32}... | collective-permute-start | bytes 393224 | tf_op jit(solution)/shard_map/while/body/eval_jaxpr/ppermute | solution.py:35
  257.3 1.8 convolution_add_fusion.5
  260.6 5.7 %collective-permute-start.2 = (bf16[256,256]{1,0:T(8,128)(2,1)S(1)}, bf16[256,256]{1,0:T(8,128)(2,1)S(1)}, u32[]{:S(2)}, u32[]{:S(2)}) collective-permute-start(bf16[256,256]{1,0:T(8,128)(2,1)S(1)} %copy.154), channel_id=1, source_target_pairs={{4,0},{8,4},{12,8},{16,12},{20,16},{24,20},{28,24},{32,28},{36,32}... | collective-permute-start | bytes 393224 | tf_op jit(solution)/shard_map/while/body/eval_jaxpr/ppermute | solution.py:35
  270.8 1.8 convolution_add_fusion.5
  274.1 5.7 %collective-permute-start.2 = (bf16[256,256]{1,0:T(8,128)(2,1)S(1)}, bf16[256,256]{1,0:T(8,128)(2,1)S(1)}, u32[]{:S(2)}, u32[]{:S(2)}) collective-permute-start(bf16[256,256]{1,0:T(8,128)(2,1)S(1)} %copy.154), channel_id=1, source_target_pairs={{4,0},{8,4},{12,8},{16,12},{20,16},{24,20},{28,24},{32,28},{36,32}... | collective-permute-start | bytes 393224 | tf_op jit(solution)/shard_map/while/body/eval_jaxpr/ppermute | solution.py:35
  284.3 1.8 convolution_add_fusion.5
  287.5 5.7 %collective-permute-start.2 = (bf16[256,256]{1,0:T(8,128)(2,1)S(1)}, bf16[256,256]{1,0:T(8,128)(2,1)S(1)}, u32[]{:S(2)}, u32[]{:S(2)}) collective-permute-start(bf16[256,256]{1,0:T(8,128)(2,1)S(1)} %copy.154), channel_id=1, source_target_pairs={{4,0},{8,4},{12,8},{16,12},{20,16},{24,20},{28,24},{32,28},{36,32}... | collective-permute-start | bytes 393224 | tf_op jit(solution)/shard_map/while/body/eval_jaxpr/ppermute | solution.py:35
  297.7 1.8 convolution_add_fusion.5
  301.0 5.7 %collective-permute-start.2 = (bf16[256,256]{1,0:T(8,128)(2,1)S(1)}, bf16[256,256]{1,0:T(8,128)(2,1)S(1)}, u32[]{:S(2)}, u32[]{:S(2)}) collective-permute-start(bf16[256,256]{1,0:T(8,128)(2,1)S(1)} %copy.154), channel_id=1, source_target_pairs={{4,0},{8,4},{12,8},{16,12},{20,16},{24,20},{28,24},{32,28},{36,32}... | collective-permute-start | bytes 393224 | tf_op jit(solution)/shard_map/while/body/eval_jaxpr/ppermute | solution.py:35
  311.2 1.8 convolution_add_fusion.5
  314.5 5.7 %collective-permute-start.2 = (bf16[256,256]{1,0:T(8,128)(2,1)S(1)}, bf16[256,256]{1,0:T(8,128)(2,1)S(1)}, u32[]{:S(2)}, u32[]{:S(2)}) collective-permute-start(bf16[256,256]{1,0:T(8,128)(2,1)S(1)} %copy.154), channel_id=1, source_target_pairs={{4,0},{8,4},{12,8},{16,12},{20,16},{24,20},{28,24},{32,28},{36,32}... | collective-permute-start | bytes 393224 | tf_op jit(solution)/shard_map/while/body/eval_jaxpr/ppermute | solution.py:35
  324.7 1.8 convolution_add_fusion.5
  327.9 5.7 %collective-permute-start.2 = (bf16[256,256]{1,0:T(8,128)(2,1)S(1)}, bf16[256,256]{1,0:T(8,128)(2,1)S(1)}, u32[]{:S(2)}, u32[]{:S(2)}) collective-permute-start(bf16[256,256]{1,0:T(8,128)(2,1)S(1)} %copy.154), channel_id=1, source_target_pairs={{4,0},{8,4},{12,8},{16,12},{20,16},{24,20},{28,24},{32,28},{36,32}... | collective-permute-start | bytes 393224 | tf_op jit(solution)/shard_map/while/body/eval_jaxpr/ppermute | solution.py:35
  338.1 1.8 convolution_add_fusion.5
  341.4 5.7 %collective-permute-start.2 = (bf16[256,256]{1,0:T(8,128)(2,1)S(1)}, bf16[256,256]{1,0:T(8,128)(2,1)S(1)}, u32[]{:S(2)}, u32[]{:S(2)}) collective-permute-start(bf16[256,256]{1,0:T(8,128)(2,1)S(1)} %copy.154), channel_id=1, source_target_pairs={{4,0},{8,4},{12,8},{16,12},{20,16},{24,20},{28,24},{32,28},{36,32}... | collective-permute-start | bytes 393224 | tf_op jit(solution)/shard_map/while/body/eval_jaxpr/ppermute | solution.py:35
  351.6 1.8 convolution_add_fusion.5
  354.9 5.7 %collective-permute-start.2 = (bf16[256,256]{1,0:T(8,128)(2,1)S(1)}, bf16[256,256]{1,0:T(8,128)(2,1)S(1)}, u32[]{:S(2)}, u32[]{:S(2)}) collective-permute-start(bf16[256,256]{1,0:T(8,128)(2,1)S(1)} %copy.154), channel_id=1, source_target_pairs={{4,0},{8,4},{12,8},{16,12},{20,16},{24,20},{28,24},{32,28},{36,32}... | collective-permute-start | bytes 393224 | tf_op jit(solution)/shard_map/while/body/eval_jaxpr/ppermute | solution.py:35
  365.1 1.8 convolution_add_fusion.5
  368.3 5.7 %collective-permute-start.2 = (bf16[256,256]{1,0:T(8,128)(2,1)S(1)}, bf16[256,256]{1,0:T(8,128)(2,1)S(1)}, u32[]{:S(2)}, u32[]{:S(2)}) collective-permute-start(bf16[256,256]{1,0:T(8,128)(2,1)S(1)} %copy.154), channel_id=1, source_target_pairs={{4,0},{8,4},{12,8},{16,12},{20,16},{24,20},{28,24},{32,28},{36,32}... | collective-permute-start | bytes 393224 | tf_op jit(solution)/shard_map/while/body/eval_jaxpr/ppermute | solution.py:35
  378.5 1.8 convolution_add_fusion.5
  381.8 5.7 %collective-permute-start.2 = (bf16[256,256]{1,0:T(8,128)(2,1)S(1)}, bf16[256,256]{1,0:T(8,128)(2,1)S(1)}, u32[]{:S(2)}, u32[]{:S(2)}) collective-permute-start(bf16[256,256]{1,0:T(8,128)(2,1)S(1)} %copy.154), channel_id=1, source_target_pairs={{4,0},{8,4},{12,8},{16,12},{20,16},{24,20},{28,24},{32,28},{36,32}... | collective-permute-start | bytes 393224 | tf_op jit(solution)/shard_map/while/body/eval_jaxpr/ppermute | solution.py:35
  395.2 5.7 %collective-permute-start.2 = (bf16[256,256]{1,0:T(8,128)(2,1)S(1)}, bf16[256,256]{1,0:T(8,128)(2,1)S(1)}, u32[]{:S(2)}, u32[]{:S(2)}) collective-permute-start(bf16[256,256]{1,0:T(8,128)(2,1)S(1)} %copy.154), channel_id=1, source_target_pairs={{4,0},{8,4},{12,8},{16,12},{20,16},{24,20},{28,24},{32,28},{36,32}... | collective-permute-start | bytes 393224 | tf_op jit(solution)/shard_map/while/body/eval_jaxpr/ppermute | solution.py:35
  405.5 1.8 convolution_add_fusion.5
  408.7 5.7 %collective-permute-start.2 = (bf16[256,256]{1,0:T(8,128)(2,1)S(1)}, bf16[256,256]{1,0:T(8,128)(2,1)S(1)}, u32[]{:S(2)}, u32[]{:S(2)}) collective-permute-start(bf16[256,256]{1,0:T(8,128)(2,1)S(1)} %copy.154), channel_id=1, source_target_pairs={{4,0},{8,4},{12,8},{16,12},{20,16},{24,20},{28,24},{32,28},{36,32}... | collective-permute-start | bytes 393224 | tf_op jit(solution)/shard_map/while/body/eval_jaxpr/ppermute | solution.py:35
  422.2 5.7 %collective-permute-start.2 = (bf16[256,256]{1,0:T(8,128)(2,1)S(1)}, bf16[256,256]{1,0:T(8,128)(2,1)S(1)}, u32[]{:S(2)}, u32[]{:S(2)}) collective-permute-start(bf16[256,256]{1,0:T(8,128)(2,1)S(1)} %copy.154), channel_id=1, source_target_pairs={{4,0},{8,4},{12,8},{16,12},{20,16},{24,20},{28,24},{32,28},{36,32}... | collective-permute-start | bytes 393224 | tf_op jit(solution)/shard_map/while/body/eval_jaxpr/ppermute | solution.py:35
  435.6 5.7 %collective-permute-start.2 = (bf16[256,256]{1,0:T(8,128)(2,1)S(1)}, bf16[256,256]{1,0:T(8,128)(2,1)S(1)}, u32[]{:S(2)}, u32[]{:S(2)}) collective-permute-start(bf16[256,256]{1,0:T(8,128)(2,1)S(1)} %copy.154), channel_id=1, source_target_pairs={{4,0},{8,4},{12,8},{16,12},{20,16},{24,20},{28,24},{32,28},{36,32}... | collective-permute-start | bytes 393224 | tf_op jit(solution)/shard_map/while/body/eval_jaxpr/ppermute | solution.py:35
  449.1 5.7 %collective-permute-start.2 = (bf16[256,256]{1,0:T(8,128)(2,1)S(1)}, bf16[256,256]{1,0:T(8,128)(2,1)S(1)}, u32[]{:S(2)}, u32[]{:S(2)}) collective-permute-start(bf16[256,256]{1,0:T(8,128)(2,1)S(1)} %copy.154), channel_id=1, source_target_pairs={{4,0},{8,4},{12,8},{16,12},{20,16},{24,20},{28,24},{32,28},{36,32}... | collective-permute-start | bytes 393224 | tf_op jit(solution)/shard_map/while/body/eval_jaxpr/ppermute | solution.py:35
  466.2 5.8 %convolution_convert_fusion = bf16[256,4096]{1,0:T(8,128)(2,1)S(1)} fusion(bf16[256,1024]{0,1:T(8,128)(2,1)S(1)} %bitcast.124, bf16[1024,4096]{1,0:T(8,128)(2,1)} %param.14), kind=kOutput, calls=%fused_computation.50 | convolution fusion | flops 2148532224 | bytes 11010048 | tf_op jit(solution)/shard_map/dot_general | solution.py:151
  473.5 39.5 %all-to-all-start.1 = ((bf16[4,1024,256]{1,2,0:T(8,128)(2,1)}), bf16[4,1024,256]{1,2,0:T(8,128)(2,1)S(1)}, u32[]{:S(2)}, u32[]{:S(2)}) async-start(bf16[4,1024,256]{1,2,0:T(8,128)(2,1)} %bitcast.123), calls=%async_computation.1 | async-start | bytes 4194304 | tf_op jit(solution)/shard_map/all_to_all | solution.py:45
  513.8 25.5 %all-to-all-done.1 = bf16[4,1024,256]{1,2,0:T(8,128)(2,1)S(1)} async-done(((bf16[4,1024,256]{1,2,0:T(8,128)(2,1)}), bf16[4,1024,256]{1,2,0:T(8,128)(2,1)S(1)}, u32[]{:S(2)}, u32[]{:S(2)}) %all-to-all-start.1) | async-done | bytes 2097184 | tf_op jit(solution)/shard_map/all_to_all | solution.py:45
  (850 shorter events, 204.3 us)
Async XLA Ops:
  2.7 33.0 %all-to-all-start = ((bf16[4,256,1024]{1,2,0:T(8,128)(2,1)}), bf16[4,256,1024]{1,2,0:T(8,128)(2,1)S(1)}, u32[]{:S(2)}, u32[]{:S(2)}) async-start(bf16[4,256,1024]{1,2,0:T(8,128)(2,1)} %broadcast_in_dim.152), calls=%async_computation | async-start | bytes 4194304 | tf_op jit(solution)/shard_map/all_to_all | solution.py:18
  43.8 13.4 %collective-permute-start = (bf16[256,256]{1,0:T(8,128)(2,1)S(1)}, bf16[256,256]{1,0:T(8,128)(2,1)S(1)}, u32[]{:S(2)}, u32[]{:S(2)}) collective-permute-start(bf16[256,256]{1,0:T(8,128)(2,1)S(1)} %copy.152), channel_id=1, source_target_pairs={{124,0},{0,4},{4,8},{8,12},{12,16},{16,20},{20,24},{24,28},{28,32}... | collective-permute-start | bytes 393224 | tf_op jit(solution)/shard_map/while/body/eval_jaxpr/ppermute | solution.py:35
  45.1 12.1 %collective-permute-start.1 = (bf16[256,256]{1,0:T(8,128)(2,1)S(1)}, bf16[256,256]{1,0:T(8,128)(2,1)S(1)}, u32[]{:S(2)}, u32[]{:S(2)}) collective-permute-start(bf16[256,256]{1,0:T(8,128)(2,1)S(1)} %copy.153), channel_id=1, source_target_pairs={{124,0},{0,4},{4,8},{8,12},{12,16},{16,20},{20,24},{24,28},{28,32}... | collective-permute-start | bytes 393224 | tf_op jit(solution)/shard_map/while/body/eval_jaxpr/ppermute | solution.py:35
  57.2 13.4 %collective-permute-start = (bf16[256,256]{1,0:T(8,128)(2,1)S(1)}, bf16[256,256]{1,0:T(8,128)(2,1)S(1)}, u32[]{:S(2)}, u32[]{:S(2)}) collective-permute-start(bf16[256,256]{1,0:T(8,128)(2,1)S(1)} %copy.152), channel_id=1, source_target_pairs={{124,0},{0,4},{4,8},{8,12},{12,16},{16,20},{20,24},{24,28},{28,32}... | collective-permute-start | bytes 393224 | tf_op jit(solution)/shard_map/while/body/eval_jaxpr/ppermute | solution.py:35
  58.5 12.1 %collective-permute-start.1 = (bf16[256,256]{1,0:T(8,128)(2,1)S(1)}, bf16[256,256]{1,0:T(8,128)(2,1)S(1)}, u32[]{:S(2)}, u32[]{:S(2)}) collective-permute-start(bf16[256,256]{1,0:T(8,128)(2,1)S(1)} %copy.153), channel_id=1, source_target_pairs={{124,0},{0,4},{4,8},{8,12},{12,16},{16,20},{20,24},{24,28},{28,32}... | collective-permute-start | bytes 393224 | tf_op jit(solution)/shard_map/while/body/eval_jaxpr/ppermute | solution.py:35
  70.7 13.4 %collective-permute-start = (bf16[256,256]{1,0:T(8,128)(2,1)S(1)}, bf16[256,256]{1,0:T(8,128)(2,1)S(1)}, u32[]{:S(2)}, u32[]{:S(2)}) collective-permute-start(bf16[256,256]{1,0:T(8,128)(2,1)S(1)} %copy.152), channel_id=1, source_target_pairs={{124,0},{0,4},{4,8},{8,12},{12,16},{16,20},{20,24},{24,28},{28,32}... | collective-permute-start | bytes 393224 | tf_op jit(solution)/shard_map/while/body/eval_jaxpr/ppermute | solution.py:35
  72.0 12.1 %collective-permute-start.1 = (bf16[256,256]{1,0:T(8,128)(2,1)S(1)}, bf16[256,256]{1,0:T(8,128)(2,1)S(1)}, u32[]{:S(2)}, u32[]{:S(2)}) collective-permute-start(bf16[256,256]{1,0:T(8,128)(2,1)S(1)} %copy.153), channel_id=1, source_target_pairs={{124,0},{0,4},{4,8},{8,12},{12,16},{16,20},{20,24},{24,28},{28,32}... | collective-permute-start | bytes 393224 | tf_op jit(solution)/shard_map/while/body/eval_jaxpr/ppermute | solution.py:35
  84.2 13.4 %collective-permute-start = (bf16[256,256]{1,0:T(8,128)(2,1)S(1)}, bf16[256,256]{1,0:T(8,128)(2,1)S(1)}, u32[]{:S(2)}, u32[]{:S(2)}) collective-permute-start(bf16[256,256]{1,0:T(8,128)(2,1)S(1)} %copy.152), channel_id=1, source_target_pairs={{124,0},{0,4},{4,8},{8,12},{12,16},{16,20},{20,24},{24,28},{28,32}... | collective-permute-start | bytes 393224 | tf_op jit(solution)/shard_map/while/body/eval_jaxpr/ppermute | solution.py:35
  85.4 12.1 %collective-permute-start.1 = (bf16[256,256]{1,0:T(8,128)(2,1)S(1)}, bf16[256,256]{1,0:T(8,128)(2,1)S(1)}, u32[]{:S(2)}, u32[]{:S(2)}) collective-permute-start(bf16[256,256]{1,0:T(8,128)(2,1)S(1)} %copy.153), channel_id=1, source_target_pairs={{124,0},{0,4},{4,8},{8,12},{12,16},{16,20},{20,24},{24,28},{28,32}... | collective-permute-start | bytes 393224 | tf_op jit(solution)/shard_map/while/body/eval_jaxpr/ppermute | solution.py:35
  97.6 13.4 %collective-permute-start = (bf16[256,256]{1,0:T(8,128)(2,1)S(1)}, bf16[256,256]{1,0:T(8,128)(2,1)S(1)}, u32[]{:S(2)}, u32[]{:S(2)}) collective-permute-start(bf16[256,256]{1,0:T(8,128)(2,1)S(1)} %copy.152), channel_id=1, source_target_pairs={{124,0},{0,4},{4,8},{8,12},{12,16},{16,20},{20,24},{24,28},{28,32}... | collective-permute-start | bytes 393224 | tf_op jit(solution)/shard_map/while/body/eval_jaxpr/ppermute | solution.py:35
  98.9 12.1 %collective-permute-start.1 = (bf16[256,256]{1,0:T(8,128)(2,1)S(1)}, bf16[256,256]{1,0:T(8,128)(2,1)S(1)}, u32[]{:S(2)}, u32[]{:S(2)}) collective-permute-start(bf16[256,256]{1,0:T(8,128)(2,1)S(1)} %copy.153), channel_id=1, source_target_pairs={{124,0},{0,4},{4,8},{8,12},{12,16},{16,20},{20,24},{24,28},{28,32}... | collective-permute-start | bytes 393224 | tf_op jit(solution)/shard_map/while/body/eval_jaxpr/ppermute | solution.py:35
  111.1 13.4 %collective-permute-start = (bf16[256,256]{1,0:T(8,128)(2,1)S(1)}, bf16[256,256]{1,0:T(8,128)(2,1)S(1)}, u32[]{:S(2)}, u32[]{:S(2)}) collective-permute-start(bf16[256,256]{1,0:T(8,128)(2,1)S(1)} %copy.152), channel_id=1, source_target_pairs={{124,0},{0,4},{4,8},{8,12},{12,16},{16,20},{20,24},{24,28},{28,32}... | collective-permute-start | bytes 393224 | tf_op jit(solution)/shard_map/while/body/eval_jaxpr/ppermute | solution.py:35
  112.4 12.1 %collective-permute-start.1 = (bf16[256,256]{1,0:T(8,128)(2,1)S(1)}, bf16[256,256]{1,0:T(8,128)(2,1)S(1)}, u32[]{:S(2)}, u32[]{:S(2)}) collective-permute-start(bf16[256,256]{1,0:T(8,128)(2,1)S(1)} %copy.153), channel_id=1, source_target_pairs={{124,0},{0,4},{4,8},{8,12},{12,16},{16,20},{20,24},{24,28},{28,32}... | collective-permute-start | bytes 393224 | tf_op jit(solution)/shard_map/while/body/eval_jaxpr/ppermute | solution.py:35
  124.6 13.4 %collective-permute-start = (bf16[256,256]{1,0:T(8,128)(2,1)S(1)}, bf16[256,256]{1,0:T(8,128)(2,1)S(1)}, u32[]{:S(2)}, u32[]{:S(2)}) collective-permute-start(bf16[256,256]{1,0:T(8,128)(2,1)S(1)} %copy.152), channel_id=1, source_target_pairs={{124,0},{0,4},{4,8},{8,12},{12,16},{16,20},{20,24},{24,28},{28,32}... | collective-permute-start | bytes 393224 | tf_op jit(solution)/shard_map/while/body/eval_jaxpr/ppermute | solution.py:35
  125.8 12.1 %collective-permute-start.1 = (bf16[256,256]{1,0:T(8,128)(2,1)S(1)}, bf16[256,256]{1,0:T(8,128)(2,1)S(1)}, u32[]{:S(2)}, u32[]{:S(2)}) collective-permute-start(bf16[256,256]{1,0:T(8,128)(2,1)S(1)} %copy.153), channel_id=1, source_target_pairs={{124,0},{0,4},{4,8},{8,12},{12,16},{16,20},{20,24},{24,28},{28,32}... | collective-permute-start | bytes 393224 | tf_op jit(solution)/shard_map/while/body/eval_jaxpr/ppermute | solution.py:35
  138.0 13.4 %collective-permute-start = (bf16[256,256]{1,0:T(8,128)(2,1)S(1)}, bf16[256,256]{1,0:T(8,128)(2,1)S(1)}, u32[]{:S(2)}, u32[]{:S(2)}) collective-permute-start(bf16[256,256]{1,0:T(8,128)(2,1)S(1)} %copy.152), channel_id=1, source_target_pairs={{124,0},{0,4},{4,8},{8,12},{12,16},{16,20},{20,24},{24,28},{28,32}... | collective-permute-start | bytes 393224 | tf_op jit(solution)/shard_map/while/body/eval_jaxpr/ppermute | solution.py:35
  139.3 12.1 %collective-permute-start.1 = (bf16[256,256]{1,0:T(8,128)(2,1)S(1)}, bf16[256,256]{1,0:T(8,128)(2,1)S(1)}, u32[]{:S(2)}, u32[]{:S(2)}) collective-permute-start(bf16[256,256]{1,0:T(8,128)(2,1)S(1)} %copy.153), channel_id=1, source_target_pairs={{124,0},{0,4},{4,8},{8,12},{12,16},{16,20},{20,24},{24,28},{28,32}... | collective-permute-start | bytes 393224 | tf_op jit(solution)/shard_map/while/body/eval_jaxpr/ppermute | solution.py:35
  151.5 13.4 %collective-permute-start = (bf16[256,256]{1,0:T(8,128)(2,1)S(1)}, bf16[256,256]{1,0:T(8,128)(2,1)S(1)}, u32[]{:S(2)}, u32[]{:S(2)}) collective-permute-start(bf16[256,256]{1,0:T(8,128)(2,1)S(1)} %copy.152), channel_id=1, source_target_pairs={{124,0},{0,4},{4,8},{8,12},{12,16},{16,20},{20,24},{24,28},{28,32}... | collective-permute-start | bytes 393224 | tf_op jit(solution)/shard_map/while/body/eval_jaxpr/ppermute | solution.py:35
  152.8 12.1 %collective-permute-start.1 = (bf16[256,256]{1,0:T(8,128)(2,1)S(1)}, bf16[256,256]{1,0:T(8,128)(2,1)S(1)}, u32[]{:S(2)}, u32[]{:S(2)}) collective-permute-start(bf16[256,256]{1,0:T(8,128)(2,1)S(1)} %copy.153), channel_id=1, source_target_pairs={{124,0},{0,4},{4,8},{8,12},{12,16},{16,20},{20,24},{24,28},{28,32}... | collective-permute-start | bytes 393224 | tf_op jit(solution)/shard_map/while/body/eval_jaxpr/ppermute | solution.py:35
  164.9 13.4 %collective-permute-start = (bf16[256,256]{1,0:T(8,128)(2,1)S(1)}, bf16[256,256]{1,0:T(8,128)(2,1)S(1)}, u32[]{:S(2)}, u32[]{:S(2)}) collective-permute-start(bf16[256,256]{1,0:T(8,128)(2,1)S(1)} %copy.152), channel_id=1, source_target_pairs={{124,0},{0,4},{4,8},{8,12},{12,16},{16,20},{20,24},{24,28},{28,32}... | collective-permute-start | bytes 393224 | tf_op jit(solution)/shard_map/while/body/eval_jaxpr/ppermute | solution.py:35
  166.2 12.1 %collective-permute-start.1 = (bf16[256,256]{1,0:T(8,128)(2,1)S(1)}, bf16[256,256]{1,0:T(8,128)(2,1)S(1)}, u32[]{:S(2)}, u32[]{:S(2)}) collective-permute-start(bf16[256,256]{1,0:T(8,128)(2,1)S(1)} %copy.153), channel_id=1, source_target_pairs={{124,0},{0,4},{4,8},{8,12},{12,16},{16,20},{20,24},{24,28},{28,32}... | collective-permute-start | bytes 393224 | tf_op jit(solution)/shard_map/while/body/eval_jaxpr/ppermute | solution.py:35
  178.4 13.4 %collective-permute-start = (bf16[256,256]{1,0:T(8,128)(2,1)S(1)}, bf16[256,256]{1,0:T(8,128)(2,1)S(1)}, u32[]{:S(2)}, u32[]{:S(2)}) collective-permute-start(bf16[256,256]{1,0:T(8,128)(2,1)S(1)} %copy.152), channel_id=1, source_target_pairs={{124,0},{0,4},{4,8},{8,12},{12,16},{16,20},{20,24},{24,28},{28,32}... | collective-permute-start | bytes 393224 | tf_op jit(solution)/shard_map/while/body/eval_jaxpr/ppermute | solution.py:35
  179.7 12.1 %collective-permute-start.1 = (bf16[256,256]{1,0:T(8,128)(2,1)S(1)}, bf16[256,256]{1,0:T(8,128)(2,1)S(1)}, u32[]{:S(2)}, u32[]{:S(2)}) collective-permute-start(bf16[256,256]{1,0:T(8,128)(2,1)S(1)} %copy.153), channel_id=1, source_target_pairs={{124,0},{0,4},{4,8},{8,12},{12,16},{16,20},{20,24},{24,28},{28,32}... | collective-permute-start | bytes 393224 | tf_op jit(solution)/shard_map/while/body/eval_jaxpr/ppermute | solution.py:35
  191.9 13.4 %collective-permute-start = (bf16[256,256]{1,0:T(8,128)(2,1)S(1)}, bf16[256,256]{1,0:T(8,128)(2,1)S(1)}, u32[]{:S(2)}, u32[]{:S(2)}) collective-permute-start(bf16[256,256]{1,0:T(8,128)(2,1)S(1)} %copy.152), channel_id=1, source_target_pairs={{124,0},{0,4},{4,8},{8,12},{12,16},{16,20},{20,24},{24,28},{28,32}... | collective-permute-start | bytes 393224 | tf_op jit(solution)/shard_map/while/body/eval_jaxpr/ppermute | solution.py:35
  193.2 12.1 %collective-permute-start.1 = (bf16[256,256]{1,0:T(8,128)(2,1)S(1)}, bf16[256,256]{1,0:T(8,128)(2,1)S(1)}, u32[]{:S(2)}, u32[]{:S(2)}) collective-permute-start(bf16[256,256]{1,0:T(8,128)(2,1)S(1)} %copy.153), channel_id=1, source_target_pairs={{124,0},{0,4},{4,8},{8,12},{12,16},{16,20},{20,24},{24,28},{28,32}... | collective-permute-start | bytes 393224 | tf_op jit(solution)/shard_map/while/body/eval_jaxpr/ppermute | solution.py:35
  205.3 13.4 %collective-permute-start = (bf16[256,256]{1,0:T(8,128)(2,1)S(1)}, bf16[256,256]{1,0:T(8,128)(2,1)S(1)}, u32[]{:S(2)}, u32[]{:S(2)}) collective-permute-start(bf16[256,256]{1,0:T(8,128)(2,1)S(1)} %copy.152), channel_id=1, source_target_pairs={{124,0},{0,4},{4,8},{8,12},{12,16},{16,20},{20,24},{24,28},{28,32}... | collective-permute-start | bytes 393224 | tf_op jit(solution)/shard_map/while/body/eval_jaxpr/ppermute | solution.py:35
  206.6 12.1 %collective-permute-start.1 = (bf16[256,256]{1,0:T(8,128)(2,1)S(1)}, bf16[256,256]{1,0:T(8,128)(2,1)S(1)}, u32[]{:S(2)}, u32[]{:S(2)}) collective-permute-start(bf16[256,256]{1,0:T(8,128)(2,1)S(1)} %copy.153), channel_id=1, source_target_pairs={{124,0},{0,4},{4,8},{8,12},{12,16},{16,20},{20,24},{24,28},{28,32}... | collective-permute-start | bytes 393224 | tf_op jit(solution)/shard_map/while/body/eval_jaxpr/ppermute | solution.py:35
  218.8 13.4 %collective-permute-start = (bf16[256,256]{1,0:T(8,128)(2,1)S(1)}, bf16[256,256]{1,0:T(8,128)(2,1)S(1)}, u32[]{:S(2)}, u32[]{:S(2)}) collective-permute-start(bf16[256,256]{1,0:T(8,128)(2,1)S(1)} %copy.152), channel_id=1, source_target_pairs={{124,0},{0,4},{4,8},{8,12},{12,16},{16,20},{20,24},{24,28},{28,32}... | collective-permute-start | bytes 393224 | tf_op jit(solution)/shard_map/while/body/eval_jaxpr/ppermute | solution.py:35
  220.1 12.1 %collective-permute-start.1 = (bf16[256,256]{1,0:T(8,128)(2,1)S(1)}, bf16[256,256]{1,0:T(8,128)(2,1)S(1)}, u32[]{:S(2)}, u32[]{:S(2)}) collective-permute-start(bf16[256,256]{1,0:T(8,128)(2,1)S(1)} %copy.153), channel_id=1, source_target_pairs={{124,0},{0,4},{4,8},{8,12},{12,16},{16,20},{20,24},{24,28},{28,32}... | collective-permute-start | bytes 393224 | tf_op jit(solution)/shard_map/while/body/eval_jaxpr/ppermute | solution.py:35
  232.3 13.4 %collective-permute-start = (bf16[256,256]{1,0:T(8,128)(2,1)S(1)}, bf16[256,256]{1,0:T(8,128)(2,1)S(1)}, u32[]{:S(2)}, u32[]{:S(2)}) collective-permute-start(bf16[256,256]{1,0:T(8,128)(2,1)S(1)} %copy.152), channel_id=1, source_target_pairs={{124,0},{0,4},{4,8},{8,12},{12,16},{16,20},{20,24},{24,28},{28,32}... | collective-permute-start | bytes 393224 | tf_op jit(solution)/shard_map/while/body/eval_jaxpr/ppermute | solution.py:35
  233.6 12.1 %collective-permute-start.1 = (bf16[256,256]{1,0:T(8,128)(2,1)S(1)}, bf16[256,256]{1,0:T(8,128)(2,1)S(1)}, u32[]{:S(2)}, u32[]{:S(2)}) collective-permute-start(bf16[256,256]{1,0:T(8,128)(2,1)S(1)} %copy.153), channel_id=1, source_target_pairs={{124,0},{0,4},{4,8},{8,12},{12,16},{16,20},{20,24},{24,28},{28,32}... | collective-permute-start | bytes 393224 | tf_op jit(solution)/shard_map/while/body/eval_jaxpr/ppermute | solution.py:35
  245.8 13.4 %collective-permute-start = (bf16[256,256]{1,0:T(8,128)(2,1)S(1)}, bf16[256,256]{1,0:T(8,128)(2,1)S(1)}, u32[]{:S(2)}, u32[]{:S(2)}) collective-permute-start(bf16[256,256]{1,0:T(8,128)(2,1)S(1)} %copy.152), channel_id=1, source_target_pairs={{124,0},{0,4},{4,8},{8,12},{12,16},{16,20},{20,24},{24,28},{28,32}... | collective-permute-start | bytes 393224 | tf_op jit(solution)/shard_map/while/body/eval_jaxpr/ppermute | solution.py:35
  247.0 12.1 %collective-permute-start.1 = (bf16[256,256]{1,0:T(8,128)(2,1)S(1)}, bf16[256,256]{1,0:T(8,128)(2,1)S(1)}, u32[]{:S(2)}, u32[]{:S(2)}) collective-permute-start(bf16[256,256]{1,0:T(8,128)(2,1)S(1)} %copy.153), channel_id=1, source_target_pairs={{124,0},{0,4},{4,8},{8,12},{12,16},{16,20},{20,24},{24,28},{28,32}... | collective-permute-start | bytes 393224 | tf_op jit(solution)/shard_map/while/body/eval_jaxpr/ppermute | solution.py:35
  259.2 13.4 %collective-permute-start = (bf16[256,256]{1,0:T(8,128)(2,1)S(1)}, bf16[256,256]{1,0:T(8,128)(2,1)S(1)}, u32[]{:S(2)}, u32[]{:S(2)}) collective-permute-start(bf16[256,256]{1,0:T(8,128)(2,1)S(1)} %copy.152), channel_id=1, source_target_pairs={{124,0},{0,4},{4,8},{8,12},{12,16},{16,20},{20,24},{24,28},{28,32}... | collective-permute-start | bytes 393224 | tf_op jit(solution)/shard_map/while/body/eval_jaxpr/ppermute | solution.py:35
  260.5 12.1 %collective-permute-start.1 = (bf16[256,256]{1,0:T(8,128)(2,1)S(1)}, bf16[256,256]{1,0:T(8,128)(2,1)S(1)}, u32[]{:S(2)}, u32[]{:S(2)}) collective-permute-start(bf16[256,256]{1,0:T(8,128)(2,1)S(1)} %copy.153), channel_id=1, source_target_pairs={{124,0},{0,4},{4,8},{8,12},{12,16},{16,20},{20,24},{24,28},{28,32}... | collective-permute-start | bytes 393224 | tf_op jit(solution)/shard_map/while/body/eval_jaxpr/ppermute | solution.py:35
  272.7 13.4 %collective-permute-start = (bf16[256,256]{1,0:T(8,128)(2,1)S(1)}, bf16[256,256]{1,0:T(8,128)(2,1)S(1)}, u32[]{:S(2)}, u32[]{:S(2)}) collective-permute-start(bf16[256,256]{1,0:T(8,128)(2,1)S(1)} %copy.152), channel_id=1, source_target_pairs={{124,0},{0,4},{4,8},{8,12},{12,16},{16,20},{20,24},{24,28},{28,32}... | collective-permute-start | bytes 393224 | tf_op jit(solution)/shard_map/while/body/eval_jaxpr/ppermute | solution.py:35
  274.0 12.1 %collective-permute-start.1 = (bf16[256,256]{1,0:T(8,128)(2,1)S(1)}, bf16[256,256]{1,0:T(8,128)(2,1)S(1)}, u32[]{:S(2)}, u32[]{:S(2)}) collective-permute-start(bf16[256,256]{1,0:T(8,128)(2,1)S(1)} %copy.153), channel_id=1, source_target_pairs={{124,0},{0,4},{4,8},{8,12},{12,16},{16,20},{20,24},{24,28},{28,32}... | collective-permute-start | bytes 393224 | tf_op jit(solution)/shard_map/while/body/eval_jaxpr/ppermute | solution.py:35
  286.2 13.4 %collective-permute-start = (bf16[256,256]{1,0:T(8,128)(2,1)S(1)}, bf16[256,256]{1,0:T(8,128)(2,1)S(1)}, u32[]{:S(2)}, u32[]{:S(2)}) collective-permute-start(bf16[256,256]{1,0:T(8,128)(2,1)S(1)} %copy.152), channel_id=1, source_target_pairs={{124,0},{0,4},{4,8},{8,12},{12,16},{16,20},{20,24},{24,28},{28,32}... | collective-permute-start | bytes 393224 | tf_op jit(solution)/shard_map/while/body/eval_jaxpr/ppermute | solution.py:35
  287.4 12.1 %collective-permute-start.1 = (bf16[256,256]{1,0:T(8,128)(2,1)S(1)}, bf16[256,256]{1,0:T(8,128)(2,1)S(1)}, u32[]{:S(2)}, u32[]{:S(2)}) collective-permute-start(bf16[256,256]{1,0:T(8,128)(2,1)S(1)} %copy.153), channel_id=1, source_target_pairs={{124,0},{0,4},{4,8},{8,12},{12,16},{16,20},{20,24},{24,28},{28,32}... | collective-permute-start | bytes 393224 | tf_op jit(solution)/shard_map/while/body/eval_jaxpr/ppermute | solution.py:35
  299.6 13.4 %collective-permute-start = (bf16[256,256]{1,0:T(8,128)(2,1)S(1)}, bf16[256,256]{1,0:T(8,128)(2,1)S(1)}, u32[]{:S(2)}, u32[]{:S(2)}) collective-permute-start(bf16[256,256]{1,0:T(8,128)(2,1)S(1)} %copy.152), channel_id=1, source_target_pairs={{124,0},{0,4},{4,8},{8,12},{12,16},{16,20},{20,24},{24,28},{28,32}... | collective-permute-start | bytes 393224 | tf_op jit(solution)/shard_map/while/body/eval_jaxpr/ppermute | solution.py:35
  300.9 12.1 %collective-permute-start.1 = (bf16[256,256]{1,0:T(8,128)(2,1)S(1)}, bf16[256,256]{1,0:T(8,128)(2,1)S(1)}, u32[]{:S(2)}, u32[]{:S(2)}) collective-permute-start(bf16[256,256]{1,0:T(8,128)(2,1)S(1)} %copy.153), channel_id=1, source_target_pairs={{124,0},{0,4},{4,8},{8,12},{12,16},{16,20},{20,24},{24,28},{28,32}... | collective-permute-start | bytes 393224 | tf_op jit(solution)/shard_map/while/body/eval_jaxpr/ppermute | solution.py:35
  313.1 13.4 %collective-permute-start = (bf16[256,256]{1,0:T(8,128)(2,1)S(1)}, bf16[256,256]{1,0:T(8,128)(2,1)S(1)}, u32[]{:S(2)}, u32[]{:S(2)}) collective-permute-start(bf16[256,256]{1,0:T(8,128)(2,1)S(1)} %copy.152), channel_id=1, source_target_pairs={{124,0},{0,4},{4,8},{8,12},{12,16},{16,20},{20,24},{24,28},{28,32}... | collective-permute-start | bytes 393224 | tf_op jit(solution)/shard_map/while/body/eval_jaxpr/ppermute | solution.py:35
  314.4 12.1 %collective-permute-start.1 = (bf16[256,256]{1,0:T(8,128)(2,1)S(1)}, bf16[256,256]{1,0:T(8,128)(2,1)S(1)}, u32[]{:S(2)}, u32[]{:S(2)}) collective-permute-start(bf16[256,256]{1,0:T(8,128)(2,1)S(1)} %copy.153), channel_id=1, source_target_pairs={{124,0},{0,4},{4,8},{8,12},{12,16},{16,20},{20,24},{24,28},{28,32}... | collective-permute-start | bytes 393224 | tf_op jit(solution)/shard_map/while/body/eval_jaxpr/ppermute | solution.py:35
  326.5 13.4 %collective-permute-start = (bf16[256,256]{1,0:T(8,128)(2,1)S(1)}, bf16[256,256]{1,0:T(8,128)(2,1)S(1)}, u32[]{:S(2)}, u32[]{:S(2)}) collective-permute-start(bf16[256,256]{1,0:T(8,128)(2,1)S(1)} %copy.152), channel_id=1, source_target_pairs={{124,0},{0,4},{4,8},{8,12},{12,16},{16,20},{20,24},{24,28},{28,32}... | collective-permute-start | bytes 393224 | tf_op jit(solution)/shard_map/while/body/eval_jaxpr/ppermute | solution.py:35
  327.8 12.1 %collective-permute-start.1 = (bf16[256,256]{1,0:T(8,128)(2,1)S(1)}, bf16[256,256]{1,0:T(8,128)(2,1)S(1)}, u32[]{:S(2)}, u32[]{:S(2)}) collective-permute-start(bf16[256,256]{1,0:T(8,128)(2,1)S(1)} %copy.153), channel_id=1, source_target_pairs={{124,0},{0,4},{4,8},{8,12},{12,16},{16,20},{20,24},{24,28},{28,32}... | collective-permute-start | bytes 393224 | tf_op jit(solution)/shard_map/while/body/eval_jaxpr/ppermute | solution.py:35
  340.0 13.4 %collective-permute-start = (bf16[256,256]{1,0:T(8,128)(2,1)S(1)}, bf16[256,256]{1,0:T(8,128)(2,1)S(1)}, u32[]{:S(2)}, u32[]{:S(2)}) collective-permute-start(bf16[256,256]{1,0:T(8,128)(2,1)S(1)} %copy.152), channel_id=1, source_target_pairs={{124,0},{0,4},{4,8},{8,12},{12,16},{16,20},{20,24},{24,28},{28,32}... | collective-permute-start | bytes 393224 | tf_op jit(solution)/shard_map/while/body/eval_jaxpr/ppermute | solution.py:35
  341.3 12.1 %collective-permute-start.1 = (bf16[256,256]{1,0:T(8,128)(2,1)S(1)}, bf16[256,256]{1,0:T(8,128)(2,1)S(1)}, u32[]{:S(2)}, u32[]{:S(2)}) collective-permute-start(bf16[256,256]{1,0:T(8,128)(2,1)S(1)} %copy.153), channel_id=1, source_target_pairs={{124,0},{0,4},{4,8},{8,12},{12,16},{16,20},{20,24},{24,28},{28,32}... | collective-permute-start | bytes 393224 | tf_op jit(solution)/shard_map/while/body/eval_jaxpr/ppermute | solution.py:35
  353.5 13.4 %collective-permute-start = (bf16[256,256]{1,0:T(8,128)(2,1)S(1)}, bf16[256,256]{1,0:T(8,128)(2,1)S(1)}, u32[]{:S(2)}, u32[]{:S(2)}) collective-permute-start(bf16[256,256]{1,0:T(8,128)(2,1)S(1)} %copy.152), channel_id=1, source_target_pairs={{124,0},{0,4},{4,8},{8,12},{12,16},{16,20},{20,24},{24,28},{28,32}... | collective-permute-start | bytes 393224 | tf_op jit(solution)/shard_map/while/body/eval_jaxpr/ppermute | solution.py:35
  354.8 12.1 %collective-permute-start.1 = (bf16[256,256]{1,0:T(8,128)(2,1)S(1)}, bf16[256,256]{1,0:T(8,128)(2,1)S(1)}, u32[]{:S(2)}, u32[]{:S(2)}) collective-permute-start(bf16[256,256]{1,0:T(8,128)(2,1)S(1)} %copy.153), channel_id=1, source_target_pairs={{124,0},{0,4},{4,8},{8,12},{12,16},{16,20},{20,24},{24,28},{28,32}... | collective-permute-start | bytes 393224 | tf_op jit(solution)/shard_map/while/body/eval_jaxpr/ppermute | solution.py:35
  366.9 13.4 %collective-permute-start = (bf16[256,256]{1,0:T(8,128)(2,1)S(1)}, bf16[256,256]{1,0:T(8,128)(2,1)S(1)}, u32[]{:S(2)}, u32[]{:S(2)}) collective-permute-start(bf16[256,256]{1,0:T(8,128)(2,1)S(1)} %copy.152), channel_id=1, source_target_pairs={{124,0},{0,4},{4,8},{8,12},{12,16},{16,20},{20,24},{24,28},{28,32}... | collective-permute-start | bytes 393224 | tf_op jit(solution)/shard_map/while/body/eval_jaxpr/ppermute | solution.py:35
  368.2 12.1 %collective-permute-start.1 = (bf16[256,256]{1,0:T(8,128)(2,1)S(1)}, bf16[256,256]{1,0:T(8,128)(2,1)S(1)}, u32[]{:S(2)}, u32[]{:S(2)}) collective-permute-start(bf16[256,256]{1,0:T(8,128)(2,1)S(1)} %copy.153), channel_id=1, source_target_pairs={{124,0},{0,4},{4,8},{8,12},{12,16},{16,20},{20,24},{24,28},{28,32}... | collective-permute-start | bytes 393224 | tf_op jit(solution)/shard_map/while/body/eval_jaxpr/ppermute | solution.py:35
  380.4 13.4 %collective-permute-start = (bf16[256,256]{1,0:T(8,128)(2,1)S(1)}, bf16[256,256]{1,0:T(8,128)(2,1)S(1)}, u32[]{:S(2)}, u32[]{:S(2)}) collective-permute-start(bf16[256,256]{1,0:T(8,128)(2,1)S(1)} %copy.152), channel_id=1, source_target_pairs={{124,0},{0,4},{4,8},{8,12},{12,16},{16,20},{20,24},{24,28},{28,32}... | collective-permute-start | bytes 393224 | tf_op jit(solution)/shard_map/while/body/eval_jaxpr/ppermute | solution.py:35
  381.7 12.1 %collective-permute-start.1 = (bf16[256,256]{1,0:T(8,128)(2,1)S(1)}, bf16[256,256]{1,0:T(8,128)(2,1)S(1)}, u32[]{:S(2)}, u32[]{:S(2)}) collective-permute-start(bf16[256,256]{1,0:T(8,128)(2,1)S(1)} %copy.153), channel_id=1, source_target_pairs={{124,0},{0,4},{4,8},{8,12},{12,16},{16,20},{20,24},{24,28},{28,32}... | collective-permute-start | bytes 393224 | tf_op jit(solution)/shard_map/while/body/eval_jaxpr/ppermute | solution.py:35
  393.9 13.4 %collective-permute-start = (bf16[256,256]{1,0:T(8,128)(2,1)S(1)}, bf16[256,256]{1,0:T(8,128)(2,1)S(1)}, u32[]{:S(2)}, u32[]{:S(2)}) collective-permute-start(bf16[256,256]{1,0:T(8,128)(2,1)S(1)} %copy.152), channel_id=1, source_target_pairs={{124,0},{0,4},{4,8},{8,12},{12,16},{16,20},{20,24},{24,28},{28,32}... | collective-permute-start | bytes 393224 | tf_op jit(solution)/shard_map/while/body/eval_jaxpr/ppermute | solution.py:35
  395.1 12.1 %collective-permute-start.1 = (bf16[256,256]{1,0:T(8,128)(2,1)S(1)}, bf16[256,256]{1,0:T(8,128)(2,1)S(1)}, u32[]{:S(2)}, u32[]{:S(2)}) collective-permute-start(bf16[256,256]{1,0:T(8,128)(2,1)S(1)} %copy.153), channel_id=1, source_target_pairs={{124,0},{0,4},{4,8},{8,12},{12,16},{16,20},{20,24},{24,28},{28,32}... | collective-permute-start | bytes 393224 | tf_op jit(solution)/shard_map/while/body/eval_jaxpr/ppermute | solution.py:35
  407.3 13.4 %collective-permute-start = (bf16[256,256]{1,0:T(8,128)(2,1)S(1)}, bf16[256,256]{1,0:T(8,128)(2,1)S(1)}, u32[]{:S(2)}, u32[]{:S(2)}) collective-permute-start(bf16[256,256]{1,0:T(8,128)(2,1)S(1)} %copy.152), channel_id=1, source_target_pairs={{124,0},{0,4},{4,8},{8,12},{12,16},{16,20},{20,24},{24,28},{28,32}... | collective-permute-start | bytes 393224 | tf_op jit(solution)/shard_map/while/body/eval_jaxpr/ppermute | solution.py:35
  408.6 12.1 %collective-permute-start.1 = (bf16[256,256]{1,0:T(8,128)(2,1)S(1)}, bf16[256,256]{1,0:T(8,128)(2,1)S(1)}, u32[]{:S(2)}, u32[]{:S(2)}) collective-permute-start(bf16[256,256]{1,0:T(8,128)(2,1)S(1)} %copy.153), channel_id=1, source_target_pairs={{124,0},{0,4},{4,8},{8,12},{12,16},{16,20},{20,24},{24,28},{28,32}... | collective-permute-start | bytes 393224 | tf_op jit(solution)/shard_map/while/body/eval_jaxpr/ppermute | solution.py:35
  420.8 13.4 %collective-permute-start = (bf16[256,256]{1,0:T(8,128)(2,1)S(1)}, bf16[256,256]{1,0:T(8,128)(2,1)S(1)}, u32[]{:S(2)}, u32[]{:S(2)}) collective-permute-start(bf16[256,256]{1,0:T(8,128)(2,1)S(1)} %copy.152), channel_id=1, source_target_pairs={{124,0},{0,4},{4,8},{8,12},{12,16},{16,20},{20,24},{24,28},{28,32}... | collective-permute-start | bytes 393224 | tf_op jit(solution)/shard_map/while/body/eval_jaxpr/ppermute | solution.py:35
  422.1 12.1 %collective-permute-start.1 = (bf16[256,256]{1,0:T(8,128)(2,1)S(1)}, bf16[256,256]{1,0:T(8,128)(2,1)S(1)}, u32[]{:S(2)}, u32[]{:S(2)}) collective-permute-start(bf16[256,256]{1,0:T(8,128)(2,1)S(1)} %copy.153), channel_id=1, source_target_pairs={{124,0},{0,4},{4,8},{8,12},{12,16},{16,20},{20,24},{24,28},{28,32}... | collective-permute-start | bytes 393224 | tf_op jit(solution)/shard_map/while/body/eval_jaxpr/ppermute | solution.py:35
  434.3 13.4 %collective-permute-start = (bf16[256,256]{1,0:T(8,128)(2,1)S(1)}, bf16[256,256]{1,0:T(8,128)(2,1)S(1)}, u32[]{:S(2)}, u32[]{:S(2)}) collective-permute-start(bf16[256,256]{1,0:T(8,128)(2,1)S(1)} %copy.152), channel_id=1, source_target_pairs={{124,0},{0,4},{4,8},{8,12},{12,16},{16,20},{20,24},{24,28},{28,32}... | collective-permute-start | bytes 393224 | tf_op jit(solution)/shard_map/while/body/eval_jaxpr/ppermute | solution.py:35
  435.5 12.1 %collective-permute-start.1 = (bf16[256,256]{1,0:T(8,128)(2,1)S(1)}, bf16[256,256]{1,0:T(8,128)(2,1)S(1)}, u32[]{:S(2)}, u32[]{:S(2)}) collective-permute-start(bf16[256,256]{1,0:T(8,128)(2,1)S(1)} %copy.153), channel_id=1, source_target_pairs={{124,0},{0,4},{4,8},{8,12},{12,16},{16,20},{20,24},{24,28},{28,32}... | collective-permute-start | bytes 393224 | tf_op jit(solution)/shard_map/while/body/eval_jaxpr/ppermute | solution.py:35
  447.7 13.4 %collective-permute-start = (bf16[256,256]{1,0:T(8,128)(2,1)S(1)}, bf16[256,256]{1,0:T(8,128)(2,1)S(1)}, u32[]{:S(2)}, u32[]{:S(2)}) collective-permute-start(bf16[256,256]{1,0:T(8,128)(2,1)S(1)} %copy.152), channel_id=1, source_target_pairs={{124,0},{0,4},{4,8},{8,12},{12,16},{16,20},{20,24},{24,28},{28,32}... | collective-permute-start | bytes 393224 | tf_op jit(solution)/shard_map/while/body/eval_jaxpr/ppermute | solution.py:35
  449.0 12.1 %collective-permute-start.1 = (bf16[256,256]{1,0:T(8,128)(2,1)S(1)}, bf16[256,256]{1,0:T(8,128)(2,1)S(1)}, u32[]{:S(2)}, u32[]{:S(2)}) collective-permute-start(bf16[256,256]{1,0:T(8,128)(2,1)S(1)} %copy.153), channel_id=1, source_target_pairs={{124,0},{0,4},{4,8},{8,12},{12,16},{16,20},{20,24},{24,28},{28,32}... | collective-permute-start | bytes 393224 | tf_op jit(solution)/shard_map/while/body/eval_jaxpr/ppermute | solution.py:35
  473.5 65.8 %all-to-all-start.1 = ((bf16[4,1024,256]{1,2,0:T(8,128)(2,1)}), bf16[4,1024,256]{1,2,0:T(8,128)(2,1)S(1)}, u32[]{:S(2)}, u32[]{:S(2)}) async-start(bf16[4,1024,256]{1,2,0:T(8,128)(2,1)} %bitcast.123), calls=%async_computation.1 | async-start | bytes 4194304 | tf_op jit(solution)/shard_map/all_to_all | solution.py:45
  (97 other events, 628.1 us)
where the time goes:
time: 542 us; the launch traced here: 541 us
  starting transfers between devices  276 us (51%)
  matrix products  146 us (27%)
  other arithmetic  50.1 us (9%)
  waiting for transfers between devices  50 us (9%)
  local copies, waits for them, and re-layouts  14.4 us (3%)
    ppermute x124, starting transfers between devices, from_behind(): return lax.ppermute(block, axis, route)  230 us
    dot_general x64, matrix products, dense_block(): jnp.einsum('vus,svg->vug', weights.astype(jnp.bfloat16), value_heads, pre...  97 us
    all_to_all x1, starting transfers between devices, sent_and_summed(): lax.all_to_all(tiles, axis, split_axis=0, concat_axis=0, tiled=True)  39.5 us
    dot_general x64, matrix products, dense_block(): jnp.einsum('sxn,lsn->sxl', grouped_queries, key_head_count, preferred_ele...  36.4 us
    reduce_sum x64, other arithmetic, dense_block(): weight_sum = weight_sum * factor + jnp.sum(weights, axis=2)  32.2 us
    all_to_all x1, waiting for transfers between devices, sent_and_summed(): lax.all_to_all(tiles, axis, split_axis=0, concat_axis=0, tiled=True)  25.5 us
    all_to_all x1, waiting for transfers between devices, from_everyone(): return lax.all_to_all(copies, axis, split_axis=0, concat_axis=0, tiled=True)  24.1 us
    lt x32, other arithmetic, dense_block(): visible = key_frames[None, None, :] < group_limits[None, :, None]  11.7 us
  transfers between devices with their start and end apart: 126, of which 2 were waited for; matrix products, arithmetic and copies ran while one was open for 33% of the time, Pallas kernels for 0%

commit v1 on v0

v1 whole, which is shorter than its diff:
```python
import functools
import math

import jax
import jax.numpy as jnp
from jax import lax
from jax.experimental import pallas as pl
from jax.experimental.pallas import tpu as pltpu
from jax.sharding import Mesh, PartitionSpec as P

HD = 128
TBLK = 64
GROUP = 4
NEG = -1e30
C = math.log2(math.e) / math.sqrt(HD)
TK = 512
CH = 128
UN = 4
PB = 2


def attn_kernel(blocks, cnt_ref, blk_ref, tile_ref, first_ref, mask_ref, bnd_ref, q_ref, k_ref, vt_ref, o_ref, st_ref, *scr):
    S = [scr[2*u:2*u+2] for u in range(UN)]; PP = [scr[2*UN+2*u:2*UN+2*u+2] for u in range(UN)]
    m_st, l_st, al_st, acc, m_c, l_c, a_c, kx, qs = scr[4*UN:]
    n = cnt_ref[0]
    m_st[...] = jnp.full_like(m_st, NEG)
    l_st[...] = jnp.zeros_like(l_st)
    al_st[...] = jnp.zeros_like(al_st)
    acc[...] = jnp.zeros_like(acc)
    m_c[...] = jnp.full_like(m_c, NEG)
    l_c[...] = jnp.zeros_like(l_c)
    a_c[...] = jnp.zeros_like(a_c)
    for h in range(2):
        for u in range(UN): PP[u][h][...] = jnp.zeros_like(PP[u][h])
    kx[blocks] = jnp.zeros((TK, HD), jnp.bfloat16)
    io = lax.broadcasted_iota(jnp.int32, (TK, HD), 0)
    @pl.loop(0, blocks)
    def _(b):
        kx[b] = jnp.where(io < bnd_ref[b], 0.0, 1.0).astype(jnp.bfloat16)
        r = pl.multiple_of(b * TBLK, TBLK)
        for h in range(2):
            for g in range(GROUP):
                qs[b, h, g*TBLK:(g+1)*TBLK, :] = q_ref[pl.ds(r, TBLK), (h*GROUP+g)*HD:(h*GROUP+g+1)*HD]
    qx = jnp.where(lax.broadcasted_iota(jnp.int32, (256, HD), 1) == 0, NEG, 0.0).astype(jnp.bfloat16)
    kx[blocks + 1, 0:256, :] = qx
    kx[blocks + 2] = jnp.ones((TK, HD), jnp.bfloat16)

    def qk(par, i, h):
        b = blk_ref[i]; t = tile_ref[i]
        lhs = jnp.concatenate([k_ref[t, :, h*HD:(h+1)*HD], kx[mask_ref[i]]], axis=1)
        rhs = jnp.concatenate([qs[b, h], kx[blocks+1, 0:256, :]], axis=1)
        S[par][h][...] = lax.dot_general(lhs, rhs, (((1,), (1,)), ((), ())), preferred_element_type=jnp.float32)

    def pv(par, i, h, late):
        b = blk_ref[i]; t = tile_ref[i]
        r = lax.dot_general(vt_ref[t, h*HD:(h+1)*HD, :], PP[par][h][...], (((1,), (0,)), ((), ())), preferred_element_type=jnp.float32)
        new = a_c[h] * al_st[par, h] + r
        a_c[h] = new
        late.append((acc, b, h, new))

    def softmax(par, i, h, late):
        b = blk_ref[i]
        first = first_ref[i] == 1
        s_ref = S[par][h]; p_ref = PP[par][h]
        mx = None
        for c in range(TK//CH):
            s = s_ref[c*CH:(c+1)*CH, :]
            v = jnp.max(s.reshape(CH//8, 8, 256), axis=0)
            mx = v if mx is None else jnp.maximum(mx, v)
        m_prev = jnp.where(first, jnp.full((1,256),NEG,jnp.float32), m_c[h])
        m_new = jnp.maximum(m_prev, jnp.max(mx, axis=0, keepdims=True))
        m_c[h] = m_new
        alpha = jnp.exp2((m_prev - m_new) * C)
        al_st[par, h] = alpha
        ls = None
        for c in range(TK//CH):
            p = jnp.exp2((s_ref[c*CH:(c+1)*CH, :] - m_new) * C)
            v = jnp.sum(p.reshape(CH//8, 8, 256), axis=0)
            ls = v if ls is None else ls + v
            p_ref[c*CH:(c+1)*CH, :] = p.astype(jnp.bfloat16)
        l_new = l_c[h] * alpha + ls
        l_c[h] = l_new
        late.append((m_st, b, h, m_new)); late.append((l_st, b, h, l_new))

    def flush(late):
        for ref, b, h, v in late:
            ref[b, h] = v

    for u in range(PB):
        for h in range(2): qk(u, PB+u, h)
    def block(base, i):
        late = []
        us = [(u, h) for u in range(PB) for h in range(2)]
        for u, h in us: qk((base+u+PB)%UN, i+u+PB, h)
        for u, h in us: pv((base+u-PB)%UN, i+u-PB, h, late)
        for u, h in us: softmax((base+u)%UN, i+u, h, late)
        flush(late)
    R = UN // PB
    def tail(base, i):
        late = []
        for u in range(PB):
            for h in range(2): pv((base+u)%UN, i+u, h, late)
        flush(late)
    @pl.loop(0, lax.div(n + R, R))
    def _(j):
        for r in range(R):
            step = j * R + r
            @pl.when(step < n)
            def _():
                block(r*PB, (step+1) * PB)
            @pl.when(step == n)
            def _():
                tail(((r-1)*PB)%UN, step * PB)
    @pl.loop(0, blocks)
    def _(b):
        for h in range(2):
            l = jnp.sum(l_st[b, h], axis=0, keepdims=True)
            o_ref[b, h] = (acc[b, h] / jnp.maximum(l, 1.0)).astype(jnp.bfloat16)
            st_ref[b, h, 0:1, :] = m_st[b, h]
            st_ref[b, h, 1:2, :] = l

def tables(nvis, NT):
    blocks = nvis.shape[0]
    tiles = (nvis + TK - 1)//TK
    ends = jnp.cumsum(tiles)
    starts = ends - tiles
    N = blocks*NT
    total = ends[-1]
    idx = jnp.arange(-PB, N+3*PB, dtype=jnp.int32)
    ii = jnp.clip(idx, 0, jnp.maximum(total-1, 0))
    blk = jnp.minimum(jnp.sum((ends[None,:] <= ii[:,None]).astype(jnp.int32), axis=1), blocks-1)
    sel = (jnp.arange(blocks)[None,:]==blk[:,None]).astype(jnp.int32)
    tile = jnp.clip(ii - jnp.sum(sel*starts[None,:],axis=1), 0, NT-1)
    real = idx < total
    rem = jnp.sum(sel*nvis[None,:],axis=1) - tile*TK
    mask = jnp.where(real, jnp.where(rem < TK, blk, blocks), blocks + 2)
    first = jnp.where(real & (tile == 0) & (idx >= 0), 1, 0)
    bnd = nvis - jnp.maximum(tiles - 1, 0)*TK
    return ((total + PB-1)//PB).reshape(1).astype(jnp.int32), blk, tile, first, mask, bnd

def attention(nvis, q, k, vt):
    blocks = nvis.shape[0]
    NT = k.shape[0]
    sm = pl.BlockSpec(memory_space=pltpu.SMEM); vm = pl.BlockSpec(memory_space=pltpu.VMEM)
    return pl.pallas_call(
        functools.partial(attn_kernel, blocks),
        out_shape=(jax.ShapeDtypeStruct((blocks,2,HD,256), jnp.bfloat16), jax.ShapeDtypeStruct((blocks,2,2,256), jnp.float32)),
        in_specs=[sm]*6+[vm]*3, out_specs=(vm,vm),
        scratch_shapes=[pltpu.VMEM((TK,256),jnp.float32)]*(2*UN) + [pltpu.VMEM((TK,256),jnp.bfloat16)]*(2*UN) + [
            pltpu.VMEM((blocks,2,1,256),jnp.float32), pltpu.VMEM((blocks,2,8,256),jnp.float32), pltpu.VMEM((UN,2,1,256),jnp.float32), pltpu.VMEM((blocks,2,HD,256),jnp.float32), pltpu.VMEM((2,1,256),jnp.float32), pltpu.VMEM((2,8,256),jnp.float32), pltpu.VMEM((2,HD,256),jnp.float32),
            pltpu.VMEM((blocks+3,TK,HD),jnp.bfloat16), pltpu.VMEM((blocks,2,256,HD),jnp.bfloat16)],
        compiler_params=pltpu.CompilerParams(vmem_limit_bytes=60*1024*1024),
        cost_estimate=pl.CostEstimate(flops=10**10, bytes_accessed=10**7, transcendentals=10**7),
    )(*tables(nvis, NT), q, k, vt)


def shards(text, wq, keys, values, wo, gate, lengths, limits):
    xi = lax.axis_index("x")
    group = lax.axis_index("zl") * 4 + lax.axis_index("y")
    rows = text.shape[0]
    heads = ("zh", "core")
    k_all = lax.all_gather(keys, ("zl", "y"))
    vt_all = lax.all_gather(values.T, ("zl", "y"))
    text_all = lax.all_gather(text, heads, axis=1, tiled=True)
    q = jnp.dot(text_all, wq, preferred_element_type=jnp.float32).astype(jnp.bfloat16)
    q_all = lax.all_gather(q, "x", axis=0, tiled=True)
    blocks = 4 * rows // TBLK
    ends = jnp.cumsum(lengths)
    lim = lax.dynamic_slice_in_dim(limits, group * blocks, blocks, 0)
    seen = jnp.sum(jnp.where(jnp.arange(lengths.shape[0])[None, :] < lim[:, None], lengths[None, :], 0), axis=1)
    first_token = (jnp.arange(8) * 4 + xi) * keys.shape[0]
    nvis = jnp.sum(jnp.clip(seen[:, None] - first_token[None, :], 0, keys.shape[0]), axis=1).astype(jnp.int32)
    o, st = attention(nvis, q_all, k_all, vt_all)
    o = lax.all_to_all(o, "x", 0, 0, tiled=True)
    st = lax.all_to_all(st, "x", 0, 0, tiled=True)
    b = rows // TBLK
    o = o.reshape(4, b, 2, HD, 4 * TBLK).astype(jnp.float32)
    st = st.reshape(4, b, 2, 2, 4 * TBLK)
    m, l = st[:, :, :, 0], st[:, :, :, 1]
    share = l * jnp.exp2((m - jnp.max(m, axis=0)) * C)
    total = jnp.maximum(jnp.sum(share, axis=0), 1.0)
    mixed = jnp.sum(o * (share / total)[:, :, :, None, :], axis=0).astype(jnp.bfloat16)
    attn = mixed.reshape(b, 2, HD, GROUP, TBLK).transpose(0, 4, 1, 3, 2).reshape(rows, -1)
    part = jnp.dot(attn, wo, preferred_element_type=jnp.float32).astype(jnp.bfloat16)
    part = part.reshape(rows, 4, -1).transpose(1, 0, 2)
    got = lax.all_to_all(part, heads, 0, 0, tiled=True)
    return (jnp.tanh(gate[0]) * got.astype(jnp.float32).sum(axis=0)).astype(jnp.bfloat16)


def solution(mesh):
    mesh = Mesh(mesh.devices.reshape(2, 4, 4, 2, 2), ("zl", "y", "x", "zh", "core"))
    seq, head = ("zl", "y", "x"), ("zh", "core")
    in_specs = (P(seq, head), P(None, head), P(seq, head), P(seq, head), P(head, None), P(), P(), P())
    return jax.shard_map(shards, mesh=mesh, in_specs=in_specs, out_specs=P(seq, head), check_vma=False)
```

time: 542 us -> 290 us (0.54)
  the two profiles are of different devices: /device:TPU:1 before, /device:TPU:56 now
where the time goes in v1:
time: 290 us; the launch traced here: 292 us
  waiting for transfers between devices  188 us (65%)
  Pallas kernels  47.8 us (16%)
  between operations  15.1 us (5%)
  matrix products  12.9 us (4%)
  blocking collectives  8.88 us (3%)
  starting transfers between devices  7.33 us (3%)
  local copies, waits for them, and re-layouts  7.26 us (3%)
  other arithmetic  5.3 us (2%)
    pallas_call x1, Pallas kernels, attention(): pl.pallas_call(functools.partial(attn_kernel, blocks), out_shape=(jax.Sha...  47.8 us
    all_gather x1, waiting for transfers between devices, shards(): k_all = lax.all_gather(keys, ('zl', 'y'))  38.2 us
    all_gather x1, waiting for transfers between devices, shards(): q_all = lax.all_gather(q, 'x', axis=0, tiled=True)  34.1 us
    all_gather x1, waiting for transfers between devices, shards(): vt_all = lax.all_gather(values.T, ('zl', 'y'))  33.8 us
    all_gather x1, waiting for transfers between devices, shards(): text_all = lax.all_gather(text, heads, axis=1, tiled=True)  27.8 us
    all_to_all x1, waiting for transfers between devices, shards(): got = lax.all_to_all(part, heads, 0, 0, tiled=True)  26.5 us
    all_to_all x1, waiting for transfers between devices, shards(): o = lax.all_to_all(o, 'x', 0, 0, tiled=True)  25.1 us
    all_to_all x1, blocking collectives, shards(): st = lax.all_to_all(st, 'x', 0, 0, tiled=True)  8.88 us
  transfers between devices with their start and end apart: 6, of which 6 were waited for; matrix products, arithmetic and copies ran while one was open for 5% of the time, Pallas kernels for 0%

profile of v1, /device:TPU:56, one launch (start us, length us, event | category | flops | bytes accessed | tf_op | source)
XLA Modules:
  0.0 292.1 jit_solution(2908898079497141885)
XLA Ops:
  6.5 0.0 all-gather.7.cloned.1.call-start
  6.5 0.7 all-gather.7.cloned.1.call-update
  7.3 0.0 all-gather.13.cloned.1.call-start
  7.3 0.7 all-gather.13.cloned.1.call-update
  8.0 0.0 all-gather.11.cloned.1.call-start
  8.1 0.7 all-gather.11.cloned.1.call-update
  8.7 0.0 copy-start.2
  8.8 0.0 copy-start.3
  8.8 0.0 all-gather.9.cloned.1.call-start
  8.8 27.8 %all-gather.7.cloned.1.call-done = bf16[256,4096]{1,0:T(8,128)(2,1)} async-done(((bf16[256,1024]{1,0:T(8,128)(2,1)}), bf16[256,4096]{1,0:T(8,128)(2,1)}) %all-gather.7.cloned.1.call-update) | async-done | bytes 2097168 | tf_op jit(solution)/shard_map/all_gather | solution.py:164
  36.6 7.1 %convolution_convert_fusion.1 = bf16[256,1024]{1,0:T(8,128)(2,1)} fusion(bf16[256,4096]{1,0:T(8,128)(2,1)} %all-gather.7.cloned.1.call-done, bf16[4096,1024]{1,0:T(8,128)(2,1)} %param.9), kind=kOutput, calls=%fused_computation.5 | convolution fusion | flops 2147745792 | bytes 11010048 | tf_op jit(solution)/shard_map/dot_general | solution.py:165
  43.8 0.0 all-gather.9.cloned.1.call-update
  43.8 0.0 copy-done.2
  43.8 0.1 dynamic_slice.3
  43.9 0.0 copy-done.3
  43.9 0.2 select_reduce_fusion.2
  44.1 0.1 clamp_reduce_fusion
  44.2 0.1 copy.25
  44.3 0.5 slice.13
  44.8 0.1 reduce.1
  46.1 0.6 multiply_subtract_fusion
  46.7 0.1 convert_reduce_fusion.1
  46.8 0.0 copy-start
  46.8 0.1 select_reduce_fusion
  46.9 1.1 fusion.8
  48.0 0.0 copy-start.1
  48.0 1.1 and_select_fusion.first_ref
  49.1 33.8 %all-gather.13.cloned.1.call-done = bf16[2048,512]{0,1:T(8,128)(2,1)} async-done(((bf16[256,512]{0,1:T(8,128)(2,1)}), bf16[2048,512]{0,1:T(8,128)(2,1)}) %all-gather.13.cloned.1.call-update) | async-done | bytes 2097168 | tf_op jit(solution)/shard_map/all_gather | solution.py:163
  82.9 3.9 %copy.26 = bf16[2048,512]{1,0:T(8,128)(2,1)} copy(bf16[2048,512]{0,1:T(8,128)(2,1)} %all-gather.13.cloned.1.call-done) | data formatting | bytes 4194304 | tf_op jit(solution)/shard_map/all_gather | solution.py:163
  86.9 0.0 copy-done
  86.9 0.0 copy-done.1
  86.9 38.2 %all-gather.11.cloned.1.call-done = bf16[4096,256]{1,0:T(8,128)(2,1)} async-done(((bf16[512,256]{1,0:T(8,128)(2,1)}), bf16[4096,256]{1,0:T(8,128)(2,1)}) %all-gather.11.cloned.1.call-update) | async-done | bytes 2097168 | tf_op jit(solution)/shard_map/all_gather | solution.py:162
  125.1 34.1 %all-gather.9.cloned.1.call-done.q_ref = bf16[1024,1024]{1,0:T(8,128)(2,1)} async-done(((bf16[256,1024]{1,0:T(8,128)(2,1)}), bf16[1024,1024]{1,0:T(8,128)(2,1)}) %all-gather.9.cloned.1.call-update) | async-done | bytes 2097168 | tf_op jit(solution)/shard_map/all_gather | solution.py:166
  159.2 47.8 %shard_map.82 = (bf16[16,2,128,256]{3,2,1,0:T(8,128)(2,1)}, f32[16,2,2,256]{3,2,1,0:T(2,128)}) custom-call(s32[1]{0:T(128)} %bitcast.3.cnt_ref, s32[136]{0:T(256)} %copy-done, s32[136]{0:T(256)} %copy-done.1, s32[136]{0:T(256)} %and_select_fusion.first_ref, s32[136]{0:T(256)} %get-tuple-element.13.mask_ref, s32[16]{0:T(128)} %get-tuple-element.11.bnd_ref, ...), custom_call_target="tpu_custom_call" | custom-call | flops 10000000000 | bytes 10000000 | tf_op jit(solution)/shard_map/pallas_call | solution.py:145
  207.0 8.9 %all_to_all.15 = f32[16,2,2,256]{3,2,1,0:T(2,128)S(1)} all-to-all(f32[16,2,2,256]{3,2,1,0:T(2,128)} %get-tuple-element.8), channel_id=1, replica_groups=mesh['zl'=2,'y'=4,'x'=4,'zh'=2,'core'=2] {'x'}, dimensions={0} | all-to-all | bytes 131072 | tf_op jit(solution)/shard_map/all_to_all | solution.py:175
  215.8 3.6 %all-to-all-start = ((bf16[16,2,128,256]{3,2,1,0:T(8,128)(2,1)}), bf16[16,2,128,256]{3,2,1,0:T(8,128)(2,1)S(1)}, u32[]{:S(2)}, u32[]{:S(2)}) async-start(bf16[16,2,128,256]{3,2,1,0:T(8,128)(2,1)} %get-tuple-element.7), calls=%async_computation | async-start | bytes 4194304 | tf_op jit(solution)/shard_map/all_to_all | solution.py:174
  219.5 0.1 slice_reduce_fusion
  219.5 0.1 fusion.7
  219.7 25.1 %all-to-all-done = bf16[16,2,128,256]{3,2,1,0:T(8,128)(2,1)S(1)} async-done(((bf16[16,2,128,256]{3,2,1,0:T(8,128)(2,1)}), bf16[16,2,128,256]{3,2,1,0:T(8,128)(2,1)S(1)}, u32[]{:S(2)}, u32[]{:S(2)}) %all-to-all-start) | async-done | bytes 2097184 | tf_op jit(solution)/shard_map/all_to_all | solution.py:174
  244.7 0.4 fusion
  245.2 0.3 copy.29
  245.4 0.4 copy.30
  245.9 0.4 reshape.127
  246.2 5.7 %convolution_convert_fusion = bf16[256,4096]{1,0:T(8,128)(2,1)S(1)} fusion(bf16[256,1024]{1,0:T(8,128)(2,1)S(1)} %reshape.127, bf16[1024,4096]{1,0:T(8,128)(2,1)} %param.12), kind=kOutput, calls=%fused_computation | convolution fusion | flops 2148532224 | bytes 11010048 | tf_op jit(solution)/shard_map/dot_general | solution.py:184
  251.9 1.6 copy.50
  253.5 3.6 %all-to-all-start.2 = ((bf16[4,256,1024]{2,1,0:T(8,128)(2,1)}), bf16[4,256,1024]{2,1,0:T(8,128)(2,1)S(1)}, u32[]{:S(2)}, u32[]{:S(2)}) async-start(bf16[4,256,1024]{2,1,0:T(8,128)(2,1)} %bitcast.48), calls=%async_computation.2 | async-start | bytes 4194304 | tf_op jit(solution)/shard_map/all_to_all | solution.py:186
  257.8 26.5 %all-to-all-done.2 = bf16[4,256,1024]{2,1,0:T(8,128)(2,1)S(1)} async-done(((bf16[4,256,1024]{2,1,0:T(8,128)(2,1)}), bf16[4,256,1024]{2,1,0:T(8,128)(2,1)S(1)}, u32[]{:S(2)}, u32[]{:S(2)}) %all-to-all-start.2) | async-done | bytes 2097184 | tf_op jit(solution)/shard_map/all_to_all | solution.py:186
  284.3 0.4 convert_reduce_fusion
  284.6 0.9 multiply_convert_fusion
  (8 shorter events, 0.1 us)
Async XLA Ops:
  6.5 30.1 %all-gather.7.cloned.1.call-start = ((), (), s32[]{:S(2)}) async-start(), calls=%async_computation.3 | async-start | bytes 2621440 | tf_op jit(solution)/shard_map/all_gather | solution.py:164
  7.3 75.7 %all-gather.13.cloned.1.call-start = ((), (), s32[]{:S(2)}) async-start(), calls=%async_computation.6 | async-start | bytes 2359296 | tf_op jit(solution)/shard_map/all_gather | solution.py:163
  8.0 117.1 %all-gather.11.cloned.1.call-start = ((), (), s32[]{:S(2)}) async-start(), calls=%async_computation.5 | async-start | bytes 2359296 | tf_op jit(solution)/shard_map/all_gather | solution.py:162
  8.7 35.1 %copy-start.2 = (s32[128]{0:T(128)S(1)}, s32[128]{0:T(128)}, u32[]{:S(2)}) copy-start(s32[128]{0:T(128)} %param.15) | copy-start | bytes 1540
  8.8 35.2 %copy-start.3 = (s32[64]{0:T(128)S(1)}, s32[64]{0:T(128)}, u32[]{:S(2)}) copy-start(s32[64]{0:T(128)} %param.14) | copy-start | bytes 772
  8.8 150.4 %all-gather.9.cloned.1.call-start = ((), (), s32[]{:S(2)}) async-start(), calls=%async_computation.4 | async-start | bytes 2621440 | tf_op jit(solution)/shard_map/all_gather | solution.py:166
  46.8 40.0 %copy-start = (s32[136]{0:T(256)}, s32[136]{0:T(256)S(1)}, u32[]{:S(2)}) copy-start(s32[136]{0:T(256)S(1)} %broadcast_minimum_fusion.blk_ref) | copy-start | bytes 1636
  48.0 38.8 %copy-start.1 = (s32[136]{0:T(256)}, s32[136]{0:T(256)S(1)}, u32[]{:S(2)}) copy-start(s32[136]{0:T(256)S(1)} %get-tuple-element.14.tile_ref) | copy-start | bytes 1636
  215.8 28.9 %all-to-all-start = ((bf16[16,2,128,256]{3,2,1,0:T(8,128)(2,1)}), bf16[16,2,128,256]{3,2,1,0:T(8,128)(2,1)S(1)}, u32[]{:S(2)}, u32[]{:S(2)}) async-start(bf16[16,2,128,256]{3,2,1,0:T(8,128)(2,1)} %get-tuple-element.7), calls=%async_computation | async-start | bytes 4194304 | tf_op jit(solution)/shard_map/all_to_all | solution.py:174
  253.5 30.8 %all-to-all-start.2 = ((bf16[4,256,1024]{2,1,0:T(8,128)(2,1)}), bf16[4,256,1024]{2,1,0:T(8,128)(2,1)S(1)}, u32[]{:S(2)}, u32[]{:S(2)}) async-start(bf16[4,256,1024]{2,1,0:T(8,128)(2,1)} %bitcast.48), calls=%async_computation.2 | async-start | bytes 4194304 | tf_op jit(solution)/shard_map/all_to_all | solution.py:186
Sparse Core Ops, SparseCore 0:
  9.0 27.5 all-gather.6
  38.2 44.6 all-gather.12
  84.6 40.4 all-gather.10
  126.6 32.5 all-gather.8
